TPU v7x, 32 devices: a whole 2x2x4 slice. The times are simulated.
32 devices in a mesh: ep: 16 (over z, y, x), tp: 2 (over core).
Axes of the slice: x: 2, y: 2, z: 4, core: 2. Of those that a mesh axis runs over, the one named last changes fastest.
Arguments:
- tokens: bfloat16 [2048, 3584], P('ep', 'tp'), may hold values from -6 to 6
- routes: int32 [2048, 8], P('ep'), may hold values from 0 to 15, all different within a row; in each aligned block of 128 rows (0 to 127, 128 to 255, ...) at most 72 rows name the same one
- gate_levels: int32 [2048, 8], P('ep'), may hold values from 1 to 255
- w_gate: bfloat16 [16, 3584, 1024], P('ep', 'tp'), may hold values from -0.09375 to 0.09375
- w_up: bfloat16 [16, 3584, 1024], P('ep', 'tp'), may hold values from -0.09375 to 0.09375
- w_down: bfloat16 [16, 1024, 3584], P('ep', None, 'tp'), may hold values from -0.1875 to 0.1875
Outputs:
- mixed: bfloat16 [2048, 3584], P('ep', 'tp')
Inputs may be any that keep to these rules, and one draw needn't show every extreme that they name: `routes`: each row names 8 different experts. Among the 128 tokens of one aligned block no expert is named by more than 72 rows, and in every draw some expert is named by exactly 72 rows of some block.
All inputs are finite; a program needn't handle non-finite values.
Results may differ from a plain program's by a relative error of at most 0.0085.
Values may be sent and summed in bfloat16 or wider, within the bound.
No kernel may reach another device: no remote copies, remote signals or barrier semaphores. Data moves between devices by JAX's collectives and lax.ppermute only.
A program may use at most 64 MiB of HBM per device.

v0:
```python
import jax
import jax.numpy as jnp
from jax import lax
from jax.sharding import PartitionSpec as P


def run_expert(inputs, gate_w, up_w, down_w):
    gate_part = jnp.dot(inputs, gate_w, preferred_element_type=jnp.float32)
    up_part = jnp.dot(inputs, up_w, preferred_element_type=jnp.float32)
    gate_sum, up_sum = (
        lax.psum_scatter(gate_part, "tp", scatter_dimension=1, tiled=True),
        lax.psum_scatter(up_part, "tp", scatter_dimension=1, tiled=True),
    )
    hidden = (jax.nn.silu(gate_sum) * up_sum).astype(jnp.bfloat16)
    output = jnp.dot(
        lax.all_gather(hidden, "tp", axis=1, tiled=True), down_w, preferred_element_type=jnp.float32
    )
    return output.astype(jnp.bfloat16)


def on_device(tokens, routes, gate_levels, w_gate, w_up, w_down):
    ep_count = lax.axis_size("ep")
    tok_rows, top_count = routes.shape
    experts_here = w_gate.shape[0]
    capacity = min(tok_rows, max(2, 9 * tok_rows * top_count // (8 * experts_here * ep_count)))
    width_local = tokens.shape[1]
    slots_each = ep_count * capacity
    slots_total = experts_here * slots_each
    flat_ids = routes.reshape(-1)
    positions = jnp.arange(tok_rows * top_count, dtype=jnp.int32)
    same_expert = flat_ids[:, None] == flat_ids[None, :]
    earlier = positions[:, None] > positions[None, :]
    slot_index = jnp.sum(same_expert & earlier, axis=1)
    destination = (
        flat_ids % experts_here * ep_count + flat_ids // experts_here
    ) * capacity + slot_index
    slot_numbers = jnp.arange(slots_total, dtype=jnp.int32)
    matches = destination.reshape(tok_rows, top_count)[:, :, None] == slot_numbers[None, None, :]
    token_slots = jnp.any(matches, axis=1).astype(jnp.bfloat16)
    outgoing = jnp.einsum(
        "ts,td->sd", token_slots, tokens, preferred_element_type=jnp.float32
    ).astype(jnp.bfloat16)
    levels = gate_levels.astype(jnp.float32)
    weights = levels / jnp.sum(levels, axis=1, keepdims=True)
    weight_high = weights.astype(jnp.bfloat16).astype(jnp.float32)
    weight_low = weights - weight_high
    table_high = jnp.sum(jnp.where(matches, weight_high[:, :, None], 0.0), axis=1).astype(
        jnp.bfloat16
    )
    table_low = jnp.sum(jnp.where(matches, weight_low[:, :, None], 0.0), axis=1).astype(
        jnp.bfloat16
    )
    arrived = lax.all_to_all(
        outgoing.reshape(experts_here, ep_count, capacity, width_local),
        "ep",
        split_axis=1,
        concat_axis=1,
        tiled=True,
    )
    expert_rows = arrived.reshape(experts_here, slots_each, width_local)
    results = [run_expert(expert_rows[0], w_gate[0], w_up[0], w_down[0])]
    produced = jnp.stack(results)
    returned = lax.all_to_all(
        produced.reshape(experts_here, ep_count, capacity, width_local),
        "ep",
        split_axis=1,
        concat_axis=1,
        tiled=True,
    )
    flat_returned = returned.reshape(slots_total, width_local)
    mixed = jnp.dot(table_high, flat_returned, preferred_element_type=jnp.float32)
    mixed = mixed + jnp.dot(table_low, flat_returned, preferred_element_type=jnp.float32)
    return mixed.astype(jnp.bfloat16)


def solution(mesh):
    in_specs = (
        P("ep", "tp"),
        P("ep", None),
        P("ep", None),
        P("ep", "tp", None),
        P("ep", "tp", None),
        P("ep", None, "tp"),
    )
    out_specs = P("ep", "tp")
    return jax.shard_map(
        on_device, mesh=mesh, in_specs=in_specs, out_specs=out_specs, check_vma=False
    )
```

profile of v0, /device:TPU:14, one launch (start us, length us, event | category | flops | bytes accessed | tf_op | source)
XLA Modules:
  0.0 286.4 jit_solution(4687454529718250434)
XLA Ops:
  6.5 0.0 copy-start
  6.5 0.0 reduce-scatter.3.cloned.1.call-start
  6.5 0.8 copy.29
  7.4 0.1 eq.30
  7.5 0.5 convert_reduce_fusion
  8.0 0.1 reduce_sum.39
  8.1 0.7 multiply_add_fusion
  8.9 0.1 copy.31
  9.0 1.5 fusion
  10.4 0.0 copy-done
  10.5 1.3 convolution_convert_fusion.1
  11.7 0.0 copy-start.3
  11.8 97.5 %all_to_all.10 = bf16[1,16,72,1792]{3,2,0,1:T(8,128)(2,1)S(1)} all-to-all(bf16[1,16,72,1792]{3,2,0,1:T(8,128)(2,1)S(1)} %bitcast.26), channel_id=1, replica_groups=mesh['ep'=16,'tp'=2] {'ep'}, dimensions={1} | all-to-all | bytes 8257536 | tf_op jit(solution)/shard_map/all_to_all | solution.py:53
  109.2 0.0 copy-start.1
  109.2 2.0 copy-done.1
  111.2 0.0 copy-done.3
  111.3 6.0 %fusion.5 = f32[1152,1024]{1,0:T(8,128)} fusion(bf16[1152,1792]{1,0:T(8,128)(2,1)S(1)} %bitcast.28, bf16[1,1792,1024]{2,1,0:T(8,128)(2,1)S(1)} %copy-done.3), kind=kOutput, calls=%fused_computation.12 | convolution fusion | flops 4227858432 | bytes 12517376 | tf_op jit(solution)/shard_map/dot_general | solution.py:8
  117.2 0.0 reduce-scatter.3.cloned.1.call-update
  117.3 0.0 reduce-scatter.5.cloned.1.call-start
  117.3 10.6 %fusion.3 = f32[1152,1024]{1,0:T(8,128)} fusion(bf16[1152,1792]{1,0:T(8,128)(2,1)} %bitcast.29, bf16[1,1792,1024]{2,1,0:T(8,128)(2,1)} %param.10), kind=kOutput, calls=%fused_computation.10 | convolution fusion | flops 4227858432 | bytes 12517376 | tf_op jit(solution)/shard_map/dot_general | solution.py:9
  127.9 0.0 reduce-scatter.5.cloned.1.call-update
  127.9 0.2 all-gather.2.cloned.1.call-start
  128.1 2.0 reduce-scatter.3.cloned.1.call-done
  130.1 16.0 %reduce-scatter.5.cloned.1.call-done = f32[1152,512]{1,0:T(8,128)} async-done(((f32[1152,1024]{1,0:T(8,128)}), f32[1152,512]{1,0:T(8,128)}) %reduce-scatter.5.cloned.1.call-update) | async-done | bytes 2359312 | tf_op jit(solution)/shard_map/reduce_scatter | solution.py:12
  146.1 4.2 %multiply_convert_fusion = bf16[1152,512]{1,0:T(8,128)(2,1)} fusion(f32[1152,512]{1,0:T(8,128)} %reduce-scatter.5.cloned.1.call-done, f32[1152,512]{1,0:T(8,128)} %reduce-scatter.3.cloned.1.call-done), kind=kLoop, calls=%fused_computation.16 | loop fusion | flops 3538944 | bytes 5898240 | tf_op jit(solution)/shard_map/convert_element_type | solution.py:14
  150.3 0.0 all-gather.2.cloned.1.call-update
  150.3 12.3 %all-gather.2.cloned.1.call-done = bf16[1152,1024]{1,0:T(8,128)(2,1)} async-done(((bf16[1152,512]{1,0:T(8,128)(2,1)}), bf16[1152,1024]{1,0:T(8,128)(2,1)}) %all-gather.2.cloned.1.call-update) | async-done | bytes 2359312 | tf_op jit(solution)/shard_map/all_gather | solution.py:16
  162.6 9.1 %convolution_convert_fusion = bf16[1152,1792]{1,0:T(8,128)(2,1)} fusion(bf16[1152,1024]{1,0:T(8,128)(2,1)} %all-gather.2.cloned.1.call-done, bf16[1,1024,1792]{2,1,0:T(8,128)(2,1)} %param.11), kind=kOutput, calls=%fused_computation | convolution fusion | flops 4229922816 | bytes 10158080 | tf_op jit(solution)/shard_map/dot_general | solution.py:15
  171.8 0.0 copy-start.2
  171.8 7.1 %all-to-all-start.1 = ((bf16[1,16,72,1792]{3,2,0,1:T(8,128)(2,1)}), bf16[1,16,72,1792]{3,2,0,1:T(8,128)(2,1)}, u32[]{:S(2)}, u32[]{:S(2)}) async-start(bf16[1,16,72,1792]{3,2,0,1:T(8,128)(2,1)} %bitcast.27), calls=%async_computation.3 | async-start | bytes 8257536 | tf_op jit(solution)/shard_map/all_to_all | solution.py:63
  178.8 0.0 copy-done.2
  178.9 0.1 copy.32
  179.0 0.1 copy.35
  179.1 3.1 %select_reduce_fusion = (bf16[128,1152]{1,0:T(8,128)(2,1)S(1)}, bf16[128,1152]{1,0:T(8,128)(2,1)S(1)}) fusion(f32[128,8]{1,0:T(8,128)S(1)} %copy.35, s32[128,8]{1,0:T(8,128)S(1)} %copy.31, f32[128,8]{1,0:T(8,128)S(1)} %copy.32), kind=kLoop, calls=%fused_computation.2 | loop fusion | flops 5603328 | bytes 602112 | tf_op jit(solution)/shard_map/reduce_sum | solution.py:50
  182.2 91.0 %all-to-all-done.1 = bf16[1,16,72,1792]{3,2,0,1:T(8,128)(2,1)} async-done(((bf16[1,16,72,1792]{3,2,0,1:T(8,128)(2,1)}), bf16[1,16,72,1792]{3,2,0,1:T(8,128)(2,1)}, u32[]{:S(2)}, u32[]{:S(2)}) %all-to-all-start.1) | async-done | bytes 4128800 | tf_op jit(solution)/shard_map/all_to_all | solution.py:63
  273.2 2.9 %fusion.12 = f32[128,1792]{1,0:T(8,128)S(1)} fusion(bf16[128,1152]{1,0:T(8,128)(2,1)S(1)} %get-tuple-element.6, bf16[1152,1792]{1,0:T(8,128)(2,1)} %bitcast.8), kind=kOutput, calls=%fused_computation.25 | convolution fusion | flops 528482304 | bytes 5341184 | tf_op jit(solution)/shard_map/dot_general | solution.py:71
  276.2 3.7 %fusion.7 = bf16[128,1792]{1,0:T(8,128)(2,1)} fusion(f32[128,1792]{1,0:T(8,128)S(1)} %fusion.12, bf16[1152,1792]{1,0:T(8,128)(2,1)} %bitcast.8, bf16[128,1152]{1,0:T(8,128)(2,1)S(1)} %get-tuple-element.5), kind=kOutput, calls=%fused_computation.15 | convolution fusion | flops 528941056 | bytes 5799936 | tf_op jit(solution)/shard_map/dot_general | solution.py:72
  (3 shorter events, 0.1 us)
Async XLA Ops:
  6.5 3.9 %copy-start = (bf16[128,1792]{1,0:T(8,128)(2,1)S(1)}, bf16[128,1792]{1,0:T(8,128)(2,1)}, u32[]{:S(2)}) copy-start(bf16[128,1792]{1,0:T(8,128)(2,1)} %param.6) | copy-start | bytes 1376260
  6.5 123.6 %reduce-scatter.3.cloned.1.call-start = ((), (), s32[]{:S(2)}) async-start(), calls=%async_computation.4 | async-start | bytes 7077888 | tf_op jit(solution)/shard_map/reduce_scatter | solution.py:11
  11.7 99.5 %copy-start.3 = (bf16[1,1792,1024]{2,1,0:T(8,128)(2,1)S(1)}, bf16[1,1792,1024]{2,1,0:T(8,128)(2,1)}, u32[]{:S(2)}) copy-start(bf16[1,1792,1024]{2,1,0:T(8,128)(2,1)} %param.9) | copy-start | bytes 11010052
  109.2 2.0 copy-start.1
  117.3 28.9 %reduce-scatter.5.cloned.1.call-start = ((), (), s32[]{:S(2)}) async-start(), calls=%async_computation.5 | async-start | bytes 7077888 | tf_op jit(solution)/shard_map/reduce_scatter | solution.py:12
  127.9 34.7 %all-gather.2.cloned.1.call-start = ((), (), s32[]{:S(2)}) async-start(), calls=%async_computation.6 | async-start | bytes 3538944 | tf_op jit(solution)/shard_map/all_gather | solution.py:16
  171.8 7.1 %copy-start.2 = (s32[128,8]{0,1:T(8,128)S(1)}, s32[128,8]{0,1:T(8,128)}, u32[]{:S(2)}) copy-start(s32[128,8]{0,1:T(8,128)} %param.8) | copy-start | bytes 12292
  171.8 101.4 %all-to-all-start.1 = ((bf16[1,16,72,1792]{3,2,0,1:T(8,128)(2,1)}), bf16[1,16,72,1792]{3,2,0,1:T(8,128)(2,1)}, u32[]{:S(2)}, u32[]{:S(2)}) async-start(bf16[1,16,72,1792]{3,2,0,1:T(8,128)(2,1)} %bitcast.27), calls=%async_computation.3 | async-start | bytes 8257536 | tf_op jit(solution)/shard_map/all_to_all | solution.py:63
Sparse Core Ops, SparseCore 0:
  117.4 12.7 reduce-scatter.2
  132.4 13.6 reduce-scatter.4
  150.5 12.1 all-gather.1
where the time goes:
time: 287 us; the launch traced here: 286 us
  waiting for transfers between devices  121 us (42%)
  blocking collectives  97.5 us (34%)
  matrix products  33.6 us (12%)
  between operations  13.2 us (5%)
  other arithmetic  9.99 us (3%)
  starting transfers between devices  7.35 us (3%)
  local copies, waits for them, and re-layouts  3.42 us (1%)
    all_to_all x1, blocking collectives, on_device(): lax.all_to_all(outgoing.reshape(experts_here, ep_count, capacity, width_l...  97.5 us
    all_to_all x1, waiting for transfers between devices, on_device(): lax.all_to_all(produced.reshape(experts_here, ep_count, capacity, width_l...  91 us
    reduce_scatter x1, waiting for transfers between devices, run_expert(): lax.psum_scatter(up_part, 'tp', scatter_dimension=1, tiled=True)  16 us
    all_gather x1, waiting for transfers between devices, run_expert(): lax.all_gather(hidden, 'tp', axis=1, tiled=True)  12.3 us
    dot_general x1, matrix products, run_expert(): up_part = jnp.dot(inputs, up_w, preferred_element_type=jnp.float32)  10.6 us
    dot_general x1, matrix products, run_expert(): jnp.dot(lax.all_gather(hidden, 'tp', axis=1, tiled=True), down_w, preferr...  9.13 us
    all_to_all x1, starting transfers between devices, on_device(): lax.all_to_all(produced.reshape(experts_here, ep_count, capacity, width_l...  7.09 us
    dot_general x1, matrix products, run_expert(): gate_part = jnp.dot(inputs, gate_w, preferred_element_type=jnp.float32)  5.98 us
  transfers between devices with their start and end apart: 4, of which 4 were waited for; matrix products, arithmetic and copies ran while one was open for 5% of the time, Pallas kernels for 0%

commit v1 on v0

v1 whole, which is shorter than its diff:
```python
import jax
import jax.numpy as jnp
from jax import lax
from jax.sharding import PartitionSpec as P

F32 = jnp.float32
BF16 = jnp.bfloat16
LANES = 128


def inner_size(count):
    size = 1
    while size * size < count and count % (2 * size) == 0:
        size *= 2
    return size


def swap_sum(own, other):
    if lax.axis_size("tp") == 2:
        return own + lax.ppermute(other.astype(BF16), "tp", [(0, 1), (1, 0)]).astype(F32)
    return own


def expert(rows, w_gate, w_up, w_down):
    gate_part = jnp.dot(rows, w_gate, preferred_element_type=F32)
    up_part = jnp.dot(rows, w_up, preferred_element_type=F32)
    ff = w_gate.shape[1]
    if lax.axis_size("tp") == 2:
        half = ff // 2
        first = lax.axis_index("tp") == 0
        keep = lambda part: jnp.where(first, part[:, :half], part[:, half:])
        give = lambda part: jnp.where(first, part[:, half:], part[:, :half]).astype(BF16)
        pairs = [(0, 1), (1, 0)]
        got = lax.ppermute(jnp.concatenate([give(gate_part), give(up_part)], axis=1), "tp", pairs)
        gate_sum = keep(gate_part) + got[:, :half].astype(F32)
        up_sum = keep(up_part) + got[:, half:].astype(F32)
        hidden = (jax.nn.silu(gate_sum) * up_sum).astype(BF16)
        other = lax.ppermute(hidden, "tp", pairs)
        hidden = jnp.concatenate(
            [jnp.where(first, hidden, other), jnp.where(first, other, hidden)], axis=1
        )
    else:
        gate_sum = lax.psum_scatter(gate_part, "tp", scatter_dimension=1, tiled=True)
        up_sum = lax.psum_scatter(up_part, "tp", scatter_dimension=1, tiled=True)
        hidden = (jax.nn.silu(gate_sum) * up_sum).astype(BF16)
        hidden = lax.all_gather(hidden, "tp", axis=1, tiled=True)
    return jnp.dot(hidden, w_down, preferred_element_type=F32).astype(BF16)


def on_device(tokens, routes, gate_levels, w_gate, w_up, w_down):
    ep_count = lax.axis_size("ep")
    tok_rows, top_count = routes.shape
    assert w_gate.shape[0] == 1
    capacity = min(tok_rows, max(2, 9 * tok_rows * top_count // (8 * ep_count)))
    width = tokens.shape[1]
    inner = inner_size(ep_count)
    outer = ep_count // inner
    plane = lax.axis_index("ep") // inner
    groups = [[o * inner + i for i in range(inner)] for o in range(outer)]

    def far(step):
        return [(i, (i // inner ^ step) * inner + i % inner) for i in range(ep_count)]

    def exchange(rows):
        return lax.all_to_all(
            rows.reshape(inner, capacity, width),
            "ep",
            split_axis=0,
            concat_axis=0,
            axis_index_groups=groups,
            tiled=True,
        ).reshape(inner * capacity, width)

    marks = jnp.concatenate([routes, gate_levels], axis=1).astype(BF16)
    marks = jnp.pad(marks, ((0, 0), (0, LANES - 2 * top_count)))
    own = jnp.concatenate([tokens, marks], axis=1)
    blocks = [own] + [lax.ppermute(own, "ep", far(k)) for k in range(1, outer)]

    below = jnp.tril(jnp.ones((tok_rows, tok_rows), BF16), -1)
    experts = (plane * inner + jnp.arange(inner)).astype(F32)
    slots = jnp.arange(capacity, dtype=F32)

    def tables(block):
        ids = block[:, width : width + top_count].astype(F32)
        levels = block[:, width + top_count : width + 2 * top_count].astype(F32)
        hit = ids[:, :, None] == experts[None, None, :]
        named = jnp.any(hit, axis=1)
        slot = jnp.dot(below, named.astype(BF16), preferred_element_type=F32)
        slot = jnp.where(named, slot, -1.0)
        share = levels / jnp.sum(levels, axis=1, keepdims=True)
        share = jnp.sum(jnp.where(hit, share[:, :, None], 0.0), axis=1)
        match = slot[:, :, None] == slots[None, None, :]
        pick = match.astype(BF16).reshape(tok_rows, inner * capacity)
        mix = jnp.where(match, share[:, :, None], 0.0).astype(BF16)
        return pick, mix.reshape(tok_rows, inner * capacity)

    mixes, arrived = [], []
    for block in blocks:
        pick, mix = tables(block)
        packed = lax.dot_general(
            pick, block[:, :width], (((0,), (0,)), ((), ())), preferred_element_type=F32
        ).astype(BF16)
        mixes.append(mix)
        arrived.append(exchange(packed))

    parts = []
    for k in list(range(1, outer)) + [0]:
        produced = expert(arrived[k], w_gate[0], w_up[0], w_down[0])
        returned = exchange(produced)
        part = jnp.dot(mixes[k], returned, preferred_element_type=F32)
        if k:
            part = lax.ppermute(part.astype(BF16), "ep", far(k)).astype(F32)
        parts.append(part)
    total = parts[-1]
    for part in parts[:-1]:
        total = total + part
    return total.astype(BF16)


def solution(mesh):
    in_specs = (
        P("ep", "tp"),
        P("ep", None),
        P("ep", None),
        P("ep", "tp", None),
        P("ep", "tp", None),
        P("ep", None, "tp"),
    )
    return jax.shard_map(
        on_device, mesh=mesh, in_specs=in_specs, out_specs=P("ep", "tp"), check_vma=False
    )
```

time: 287 us -> 215 us (0.75)
  blocking collectives: 97.5 us -> 0 us
  starting transfers between devices: 7.35 us -> 48.4 us
  waiting for transfers between devices: 121 us -> 100 us
  between operations: 13.2 us -> 0.43 us
  other arithmetic: 9.99 us -> 18.7 us
  matrix products: 33.6 us -> 41.2 us
    all_to_all x1 -> x0, blocking collectives: 97.5 us -> none  [on_device(): lax.all_to_all(outgoing.reshape(experts_here, ep_count, capacity, width_l...]
    ppermute x0 -> x14, waiting for transfers between devices: none -> 54.3 us  [the longest x3 42.2 us: on_device(): blocks = [own] + [lax.ppermute(own, 'ep', far(k)) for k in range(1, outer)]]
    all_to_all x1 -> x8, waiting for transfers between devices: 91 us -> 46 us  [exchange(): lax.all_to_all(rows.reshape(inner, capacity, width), 'ep', split_axis=0,...]
    all_to_all x1 -> x8, starting transfers between devices: 7.09 us -> 39.3 us  [exchange(): lax.all_to_all(rows.reshape(inner, capacity, width), 'ep', split_axis=0,...]
    reduce_scatter x2 -> x0, waiting for transfers between devices: 18 us -> none  [the longest x1 16 us: run_expert(): lax.psum_scatter(up_part, 'tp', scatter_dimension=1, tiled=True)]
    all_gather x1 -> x0, waiting for transfers between devices: 12.3 us -> none  [run_expert(): lax.all_gather(hidden, 'tp', axis=1, tiled=True)]
    ppermute x0 -> x14, starting transfers between devices: none -> 9.1 us  [the longest x3 4.67 us: on_device(): part = lax.ppermute(part.astype(BF16), 'ep', far(k)).astype(F32)]
    dot_general x6 -> x24, matrix products: 33.6 us -> 41.2 us  [the longest x4 13.6 us: expert(): up_part = jnp.dot(rows, w_up, preferred_element_type=F32)]
  transfers between devices with their start and end apart: 4 -> 22, of which waited for: 4 -> 13; matrix products, arithmetic and copies ran while one was open for 5% -> 25% of each run, Pallas kernels for 0% -> 0%
where the time goes in v1:
time: 215 us; the launch traced here: 212 us
  waiting for transfers between devices  100 us (47%)
  starting transfers between devices  48.4 us (23%)
  matrix products  41.2 us (19%)
  other arithmetic  18.7 us (9%)
  local copies, waits for them, and re-layouts  3.09 us (1%)
    all_to_all x8, waiting for transfers between devices, exchange(): lax.all_to_all(rows.reshape(inner, capacity, width), 'ep', split_axis=0,...  46 us
    ppermute x3, waiting for transfers between devices, on_device(): blocks = [own] + [lax.ppermute(own, 'ep', far(k)) for k in range(1, outer)]  42.2 us
    all_to_all x8, starting transfers between devices, exchange(): lax.all_to_all(rows.reshape(inner, capacity, width), 'ep', split_axis=0,...  39.3 us
    dot_general x4, matrix products, expert(): up_part = jnp.dot(rows, w_up, preferred_element_type=F32)  13.6 us
    ppermute x3, waiting for transfers between devices, on_device(): part = lax.ppermute(part.astype(BF16), 'ep', far(k)).astype(F32)  12.1 us
    dot_general x4, matrix products, expert(): return jnp.dot(hidden, w_down, preferred_element_type=F32).astype(BF16)  10.9 us
    convert_element_type x4, other arithmetic, expert(): hidden = (jax.nn.silu(gate_sum) * up_sum).astype(BF16)  8.33 us
    dot_general x4, matrix products, on_device(): lax.dot_general(pick, block[:, :width], (((0,), (0,)), ((), ())), preferr...  5.64 us
  transfers between devices with their start and end apart: 22, of which 13 were waited for; matrix products, arithmetic and copies ran while one was open for 25% of the time, Pallas kernels for 0%

profile of v1, /device:TPU:14, one launch (start us, length us, event | category | flops | bytes accessed | tf_op | source)
XLA Modules:
  0.0 212.1 jit_solution(14099244903063267160)
XLA Ops:
  0.0 0.7 fusion.106
  0.7 0.7 convert_reduce_fusion.3
  1.4 1.3 copy.17
  2.7 0.5 collective-permute-start.2
  3.2 2.6 %collective-permute-start.6 = (bf16[128,1920]{0,1:T(8,128)(2,1)S(1)}, bf16[128,1920]{0,1:T(8,128)(2,1)S(1)}, u32[]{:S(2)}, u32[]{:S(2)}) collective-permute-start(bf16[128,1920]{0,1:T(8,128)(2,1)S(1)} %pad_maximum_fusion.4), channel_id=1, source_target_pairs={{0,16},{2,18},{4,20},{6,22},{8,24},{10,26},{12,28},{14,30},{16,0},... | collective-permute-start | bytes 1474568 | tf_op jit(solution)/shard_map/ppermute | solution.py:77
  5.8 0.5 collective-permute-start.10
  6.4 17.1 %collective-permute-done.2 = bf16[128,1920]{0,1:T(8,128)(2,1)S(1)} collective-permute-done((bf16[128,1920]{0,1:T(8,128)(2,1)S(1)}, bf16[128,1920]{0,1:T(8,128)(2,1)S(1)}, u32[]{:S(2)}, u32[]{:S(2)}) %collective-permute-start.2) | collective-permute-done | bytes 491552 | tf_op jit(solution)/shard_map/ppermute | solution.py:77
  23.5 15.0 %collective-permute-done.6 = bf16[128,1920]{0,1:T(8,128)(2,1)S(1)} collective-permute-done((bf16[128,1920]{0,1:T(8,128)(2,1)S(1)}, bf16[128,1920]{0,1:T(8,128)(2,1)S(1)}, u32[]{:S(2)}, u32[]{:S(2)}) %collective-permute-start.6) | collective-permute-done | bytes 491552 | tf_op jit(solution)/shard_map/ppermute | solution.py:77
  38.5 10.1 %collective-permute-done.10 = bf16[128,1920]{0,1:T(8,128)(2,1)S(1)} collective-permute-done((bf16[128,1920]{0,1:T(8,128)(2,1)S(1)}, bf16[128,1920]{0,1:T(8,128)(2,1)S(1)}, u32[]{:S(2)}, u32[]{:S(2)}) %collective-permute-start.10) | collective-permute-done | bytes 491552 | tf_op jit(solution)/shard_map/ppermute | solution.py:77
  48.9 0.2 convolution_select_fusion.2
  49.7 1.4 convolution_convert_fusion
  51.1 4.3 %all-to-all-start.6 = ((bf16[4,72,1792]{2,1,0:T(8,128)(2,1)}), bf16[4,72,1792]{2,1,0:T(8,128)(2,1)S(1)}, u32[]{:S(2)}, u32[]{:S(2)}) async-start(bf16[4,72,1792]{2,1,0:T(8,128)(2,1)} %bitcast.19), calls=%async_computation.6 | async-start | bytes 2064384 | tf_op jit(solution)/shard_map/all_to_all | solution.py:65
  55.5 0.7 fusion.78
  56.2 1.4 convolution_convert_fusion.3
  57.6 1.4 convolution_convert_fusion.1
  59.1 1.4 convolution_convert_fusion.2
  60.4 5.9 %all-to-all-done.6 = bf16[4,72,1792]{2,1,0:T(8,128)(2,1)S(1)} async-done(((bf16[4,72,1792]{2,1,0:T(8,128)(2,1)}), bf16[4,72,1792]{2,1,0:T(8,128)(2,1)S(1)}, u32[]{:S(2)}, u32[]{:S(2)}) %all-to-all-start.6) | async-done | bytes 1032224 | tf_op jit(solution)/shard_map/all_to_all | solution.py:65
  66.4 5.0 %all-to-all-start.4 = ((bf16[4,72,1792]{2,1,0:T(8,128)(2,1)}), bf16[4,72,1792]{2,1,0:T(8,128)(2,1)S(1)}, u32[]{:S(2)}, u32[]{:S(2)}) async-start(bf16[4,72,1792]{2,1,0:T(8,128)(2,1)} %bitcast.14), calls=%async_computation.4 | async-start | bytes 2064384 | tf_op jit(solution)/shard_map/all_to_all | solution.py:65
  71.4 3.4 %fusion.8 = f32[288,1024]{1,0:T(8,128)S(1)} fusion(bf16[288,1792]{1,0:T(8,128)(2,1)S(1)} %bitcast.92, bf16[1,1792,1024]{2,1,0:T(8,128)(2,1)} %param.10), kind=kOutput, calls=%fused_computation.8 | convolution fusion | flops 1056964608 | bytes 5881856 | tf_op jit(solution)/shard_map/dot_general | solution.py:26
  74.8 1.3 fusion.16
  76.2 1.1 pad_maximum_fusion.3
  77.3 5.5 %all-to-all-done.4 = bf16[4,72,1792]{2,1,0:T(8,128)(2,1)S(1)} async-done(((bf16[4,72,1792]{2,1,0:T(8,128)(2,1)}), bf16[4,72,1792]{2,1,0:T(8,128)(2,1)S(1)}, u32[]{:S(2)}, u32[]{:S(2)}) %all-to-all-start.4) | async-done | bytes 1032224 | tf_op jit(solution)/shard_map/all_to_all | solution.py:65
  82.8 5.0 %all-to-all-start.2 = ((bf16[4,72,1792]{2,1,0:T(8,128)(2,1)}), bf16[4,72,1792]{2,1,0:T(8,128)(2,1)S(1)}, u32[]{:S(2)}, u32[]{:S(2)}) async-start(bf16[4,72,1792]{2,1,0:T(8,128)(2,1)} %bitcast.9), calls=%async_computation.2 | async-start | bytes 2064384 | tf_op jit(solution)/shard_map/all_to_all | solution.py:65
  87.8 3.4 %fusion.10 = f32[288,1024]{1,0:T(8,128)S(1)} fusion(bf16[288,1792]{1,0:T(8,128)(2,1)S(1)} %bitcast.98, bf16[1,1792,1024]{2,1,0:T(8,128)(2,1)} %param.10), kind=kOutput, calls=%fused_computation.10 | convolution fusion | flops 1056964608 | bytes 5881856 | tf_op jit(solution)/shard_map/dot_general | solution.py:26
  91.3 1.3 fusion.18
  92.7 1.1 pad_maximum_fusion.2
  93.8 5.5 %all-to-all-done.2 = bf16[4,72,1792]{2,1,0:T(8,128)(2,1)S(1)} async-done(((bf16[4,72,1792]{2,1,0:T(8,128)(2,1)}), bf16[4,72,1792]{2,1,0:T(8,128)(2,1)S(1)}, u32[]{:S(2)}, u32[]{:S(2)}) %all-to-all-start.2) | async-done | bytes 1032224 | tf_op jit(solution)/shard_map/all_to_all | solution.py:65
  99.3 5.0 %all-to-all-start = ((bf16[4,72,1792]{2,1,0:T(8,128)(2,1)}), bf16[4,72,1792]{2,1,0:T(8,128)(2,1)S(1)}, u32[]{:S(2)}, u32[]{:S(2)}) async-start(bf16[4,72,1792]{2,1,0:T(8,128)(2,1)} %bitcast.1), calls=%async_computation | async-start | bytes 2064384 | tf_op jit(solution)/shard_map/all_to_all | solution.py:65
  104.3 3.4 %fusion.12 = f32[288,1024]{1,0:T(8,128)S(1)} fusion(bf16[288,1792]{1,0:T(8,128)(2,1)S(1)} %bitcast.100, bf16[1,1792,1024]{2,1,0:T(8,128)(2,1)} %param.10), kind=kOutput, calls=%fused_computation.12 | convolution fusion | flops 1056964608 | bytes 5881856 | tf_op jit(solution)/shard_map/dot_general | solution.py:26
  107.7 1.3 fusion.20
  109.1 1.1 pad_maximum_fusion.1
  110.2 5.5 %all-to-all-done = bf16[4,72,1792]{2,1,0:T(8,128)(2,1)S(1)} async-done(((bf16[4,72,1792]{2,1,0:T(8,128)(2,1)}), bf16[4,72,1792]{2,1,0:T(8,128)(2,1)S(1)}, u32[]{:S(2)}, u32[]{:S(2)}) %all-to-all-start) | async-done | bytes 1032224 | tf_op jit(solution)/shard_map/all_to_all | solution.py:65
  115.8 3.4 %fusion.14 = f32[288,1024]{1,0:T(8,128)S(1)} fusion(bf16[288,1792]{1,0:T(8,128)(2,1)S(1)} %bitcast.102, bf16[1,1792,1024]{2,1,0:T(8,128)(2,1)} %param.10), kind=kOutput, calls=%fused_computation.14 | convolution fusion | flops 1056964608 | bytes 5881856 | tf_op jit(solution)/shard_map/dot_general | solution.py:26
  119.2 1.3 fusion.22
  120.6 1.6 copy-done.3
  122.2 1.5 multiply_convert_fusion
  123.8 0.9 pad_maximum_fusion
  124.7 0.5 collective-permute-start
  125.2 2.3 %multiply_convert_fusion.1 = bf16[288,512]{1,0:T(8,128)(2,1)} fusion(f32[288,1024]{1,0:T(8,128)S(1)} %copy-done.7, f32[288,1024]{1,0:T(8,128)S(1)} %copy-done.9, bf16[288,1024]{1,0:T(8,128)(2,1)} %collective-permute-done.7, pred[]{:T(512)S(6)} %eq.154), kind=kLoop, calls=%fused_computation.63 | loop fusion | flops 1769472 | bytes 3244033 | tf_op jit(solution)/shard_map/convert_element_type | solution.py:37
  127.6 2.2 %fusion.33 = bf16[288,1792]{1,0:T(8,128)(2,1)} fusion(bf16[1,1024,1792]{2,1,0:T(8,128)(2,1)S(1)} %copy-done.19, bf16[288,512]{1,0:T(8,128)(2,1)S(1)} %get-tuple-element.24, bf16[288,512]{1,0:T(8,128)(2,1)S(1)} %get-tuple-element.23), kind=kOutput, calls=%fused_computation.27 | convolution fusion | flops 1058660352 | bytes 5292032 | tf_op jit(solution)/shard_map/dot_general | solution.py:47
  129.8 5.0 %all-to-all-start.7 = ((bf16[4,72,1792]{2,1,0:T(8,128)(2,1)}), bf16[4,72,1792]{2,1,0:T(8,128)(2,1)S(1)}, u32[]{:S(2)}, u32[]{:S(2)}) async-start(bf16[4,72,1792]{2,1,0:T(8,128)(2,1)} %bitcast.97), calls=%async_computation.7 | async-start | bytes 2064384 | tf_op jit(solution)/shard_map/all_to_all | solution.py:65
  134.8 2.6 %multiply_convert_fusion.2 = bf16[288,512]{1,0:T(8,128)(2,1)} fusion(f32[288,1024]{1,0:T(8,128)S(1)} %fusion.12, f32[288,1024]{1,0:T(8,128)} %copy-done.1, bf16[288,1024]{1,0:T(8,128)(2,1)} %collective-permute-done.3, pred[]{:T(512)S(6)} %eq.154), kind=kLoop, calls=%fused_computation.66 | loop fusion | flops 1769472 | bytes 3244033 | tf_op jit(solution)/shard_map/convert_element_type | solution.py:37
  137.6 1.1 broadcast_select_fusion.2
  138.7 2.2 %fusion.30 = bf16[288,1792]{1,0:T(8,128)(2,1)} fusion(bf16[1,1024,1792]{2,1,0:T(8,128)(2,1)S(1)} %copy-done.20, bf16[288,512]{1,0:T(8,128)(2,1)S(1)} %get-tuple-element.22, bf16[288,512]{1,0:T(8,128)(2,1)S(1)} %get-tuple-element.21), kind=kOutput, calls=%fused_computation.26 | convolution fusion | flops 1058660352 | bytes 5292032 | tf_op jit(solution)/shard_map/dot_general | solution.py:47
  140.9 6.8 %all-to-all-done.7 = bf16[4,72,1792]{2,1,0:T(8,128)(2,1)S(1)} async-done(((bf16[4,72,1792]{2,1,0:T(8,128)(2,1)}), bf16[4,72,1792]{2,1,0:T(8,128)(2,1)S(1)}, u32[]{:S(2)}, u32[]{:S(2)}) %all-to-all-start.7) | async-done | bytes 1032224 | tf_op jit(solution)/shard_map/all_to_all | solution.py:65
  147.7 5.0 %all-to-all-start.5 = ((bf16[4,72,1792]{2,1,0:T(8,128)(2,1)}), bf16[4,72,1792]{2,1,0:T(8,128)(2,1)S(1)}, u32[]{:S(2)}, u32[]{:S(2)}) async-start(bf16[4,72,1792]{2,1,0:T(8,128)(2,1)} %bitcast.94), calls=%async_computation.5 | async-start | bytes 2064384 | tf_op jit(solution)/shard_map/all_to_all | solution.py:65
  152.7 1.9 multiply_convert_fusion.3
  154.7 1.1 broadcast_select_fusion.5
  155.8 2.2 %fusion.27 = bf16[288,1792]{1,0:T(8,128)(2,1)} fusion(bf16[1,1024,1792]{2,1,0:T(8,128)(2,1)S(1)} %copy-done.21, bf16[288,512]{1,0:T(8,128)(2,1)S(1)} %get-tuple-element.20, bf16[288,512]{1,0:T(8,128)(2,1)S(1)} %get-tuple-element.19), kind=kOutput, calls=%fused_computation.25 | convolution fusion | flops 1058660352 | bytes 5292032 | tf_op jit(solution)/shard_map/dot_general | solution.py:47
  158.0 6.7 %all-to-all-done.5 = bf16[4,72,1792]{2,1,0:T(8,128)(2,1)S(1)} async-done(((bf16[4,72,1792]{2,1,0:T(8,128)(2,1)}), bf16[4,72,1792]{2,1,0:T(8,128)(2,1)S(1)}, u32[]{:S(2)}, u32[]{:S(2)}) %all-to-all-start.5) | async-done | bytes 1032224 | tf_op jit(solution)/shard_map/all_to_all | solution.py:65
  164.7 5.0 %all-to-all-start.3 = ((bf16[4,72,1792]{2,1,0:T(8,128)(2,1)}), bf16[4,72,1792]{2,1,0:T(8,128)(2,1)S(1)}, u32[]{:S(2)}, u32[]{:S(2)}) async-start(bf16[4,72,1792]{2,1,0:T(8,128)(2,1)} %bitcast.96), calls=%async_computation.3 | async-start | bytes 2064384 | tf_op jit(solution)/shard_map/all_to_all | solution.py:65
  169.7 1.0 broadcast_select_fusion.7
  170.7 4.3 %fusion.24 = bf16[288,1792]{1,0:T(8,128)(2,1)} fusion(bf16[1,1024,1792]{2,1,0:T(8,128)(2,1)} %param.11, bf16[288,512]{1,0:T(8,128)(2,1)S(1)} %get-tuple-element.18, bf16[288,512]{1,0:T(8,128)(2,1)S(1)} %get-tuple-element.17), kind=kOutput, calls=%fused_computation.24 | convolution fusion | flops 1058660352 | bytes 5292032 | tf_op jit(solution)/shard_map/dot_general | solution.py:47
  175.0 1.2 fusion.38
  176.2 1.6 collective-permute-start.13
  177.8 3.4 %all-to-all-done.3 = bf16[4,72,1792]{2,1,0:T(8,128)(2,1)S(1)} async-done(((bf16[4,72,1792]{2,1,0:T(8,128)(2,1)}), bf16[4,72,1792]{2,1,0:T(8,128)(2,1)S(1)}, u32[]{:S(2)}, u32[]{:S(2)}) %all-to-all-start.3) | async-done | bytes 1032224 | tf_op jit(solution)/shard_map/all_to_all | solution.py:65
  181.2 5.0 %all-to-all-start.1 = ((bf16[4,72,1792]{2,1,0:T(8,128)(2,1)}), bf16[4,72,1792]{2,1,0:T(8,128)(2,1)S(1)}, u32[]{:S(2)}, u32[]{:S(2)}) async-start(bf16[4,72,1792]{2,1,0:T(8,128)(2,1)} %bitcast.95), calls=%async_computation.1 | async-start | bytes 2064384 | tf_op jit(solution)/shard_map/all_to_all | solution.py:65
  186.2 1.3 fusion.37
  187.4 0.4 fusion.36
  187.9 3.1 %collective-permute-start.5 = (bf16[128,1792]{1,0:T(8,128)(2,1)S(1)}, bf16[128,1792]{1,0:T(8,128)(2,1)S(1)}, u32[]{:S(2)}, u32[]{:S(2)}) collective-permute-start(bf16[128,1792]{1,0:T(8,128)(2,1)S(1)} %fusion.36), channel_id=1, source_target_pairs={{0,8},{2,10},{4,12},{6,14},{8,0},{10,2},{12,4},{14,6},{16,24},{18,... | collective-permute-start | bytes 1376264 | tf_op jit(solution)/shard_map/ppermute | solution.py:112
  191.0 6.8 %all-to-all-done.1 = bf16[4,72,1792]{2,1,0:T(8,128)(2,1)S(1)} async-done(((bf16[4,72,1792]{2,1,0:T(8,128)(2,1)}), bf16[4,72,1792]{2,1,0:T(8,128)(2,1)S(1)}, u32[]{:S(2)}, u32[]{:S(2)}) %all-to-all-start.1) | async-done | bytes 1032224 | tf_op jit(solution)/shard_map/all_to_all | solution.py:65
  197.7 9.0 %collective-permute-done.9 = bf16[128,1792]{1,0:T(8,128)(2,1)S(1)} collective-permute-done((bf16[128,1792]{1,0:T(8,128)(2,1)}, bf16[128,1792]{1,0:T(8,128)(2,1)S(1)}, u32[]{:S(2)}, u32[]{:S(2)}) %collective-permute-start.9) | collective-permute-done | bytes 458784 | tf_op jit(solution)/shard_map/ppermute | solution.py:112
  206.7 3.1 %collective-permute-done.5 = bf16[128,1792]{1,0:T(8,128)(2,1)S(1)} collective-permute-done((bf16[128,1792]{1,0:T(8,128)(2,1)S(1)}, bf16[128,1792]{1,0:T(8,128)(2,1)S(1)}, u32[]{:S(2)}, u32[]{:S(2)}) %collective-permute-start.5) | collective-permute-done | bytes 458784 | tf_op jit(solution)/shard_map/ppermute | solution.py:112
  209.8 2.3 %add_convert_fusion = bf16[128,1792]{1,0:T(8,128)(2,1)} fusion(bf16[128,1792]{1,0:T(8,128)(2,1)} %collective-permute-done.13, bf16[128,1792]{1,0:T(8,128)(2,1)S(1)} %collective-permute-done.9, bf16[128,1792]{1,0:T(8,128)(2,1)S(1)} %collective-permute-done.5, bf16[4,72,1792]{2,1,0:T(8,128)(2,1)S(1)} %all-to-all-done.1, bf16[128,4]{0,1:T(4,128)(2,1)S(1)} %copy-done.11, ...), kind=kOutput, calls=%fused_computation.43 | convolution fusion | flops 133799936 | bytes 2870272 | tf_op jit(solution)/shard_map/dot_general | solution.py:110
  (86 shorter events, 2.2 us)
Async XLA Ops:
  2.7 20.8 %collective-permute-start.2 = (bf16[128,1920]{0,1:T(8,128)(2,1)S(1)}, bf16[128,1920]{0,1:T(8,128)(2,1)S(1)}, u32[]{:S(2)}, u32[]{:S(2)}) collective-permute-start(bf16[128,1920]{0,1:T(8,128)(2,1)S(1)} %pad_maximum_fusion.4), channel_id=1, source_target_pairs={{0,8},{2,10},{4,12},{6,14},{8,0},{10,2},{12,4},{14,6},{16,24},{18,... | collective-permute-start | bytes 1474568 | tf_op jit(solution)/shard_map/ppermute | solution.py:77
  3.2 35.3 %collective-permute-start.6 = (bf16[128,1920]{0,1:T(8,128)(2,1)S(1)}, bf16[128,1920]{0,1:T(8,128)(2,1)S(1)}, u32[]{:S(2)}, u32[]{:S(2)}) collective-permute-start(bf16[128,1920]{0,1:T(8,128)(2,1)S(1)} %pad_maximum_fusion.4), channel_id=1, source_target_pairs={{0,16},{2,18},{4,20},{6,22},{8,24},{10,26},{12,28},{14,30},{16,0},... | collective-permute-start | bytes 1474568 | tf_op jit(solution)/shard_map/ppermute | solution.py:77
  5.8 42.8 %collective-permute-start.10 = (bf16[128,1920]{0,1:T(8,128)(2,1)S(1)}, bf16[128,1920]{0,1:T(8,128)(2,1)S(1)}, u32[]{:S(2)}, u32[]{:S(2)}) collective-permute-start(bf16[128,1920]{0,1:T(8,128)(2,1)S(1)} %pad_maximum_fusion.4), channel_id=1, source_target_pairs={{0,24},{2,26},{4,28},{6,30},{8,16},{10,18},{12,20},{14,22},{16,8},... | collective-permute-start | bytes 1474568 | tf_op jit(solution)/shard_map/ppermute | solution.py:77
  51.1 5.1 %copy-start.10 = (bf16[128,1792]{1,0:T(8,128)(2,1)S(1)}, bf16[128,1792]{1,0:T(8,128)(2,1)}, u32[]{:S(2)}) copy-start(bf16[128,1792]{1,0:T(8,128)(2,1)} %param.6) | copy-start | bytes 1376260
  51.1 15.2 %all-to-all-start.6 = ((bf16[4,72,1792]{2,1,0:T(8,128)(2,1)}), bf16[4,72,1792]{2,1,0:T(8,128)(2,1)S(1)}, u32[]{:S(2)}, u32[]{:S(2)}) async-start(bf16[4,72,1792]{2,1,0:T(8,128)(2,1)} %bitcast.19), calls=%async_computation.6 | async-start | bytes 2064384 | tf_op jit(solution)/shard_map/all_to_all | solution.py:65
  66.4 16.5 %all-to-all-start.4 = ((bf16[4,72,1792]{2,1,0:T(8,128)(2,1)}), bf16[4,72,1792]{2,1,0:T(8,128)(2,1)S(1)}, u32[]{:S(2)}, u32[]{:S(2)}) async-start(bf16[4,72,1792]{2,1,0:T(8,128)(2,1)} %bitcast.14), calls=%async_computation.4 | async-start | bytes 2064384 | tf_op jit(solution)/shard_map/all_to_all | solution.py:65
  71.4 3.4 %copy-start.15 = (bf16[1,1792,1024]{2,1,0:T(8,128)(2,1)S(1)}, bf16[1,1792,1024]{2,1,0:T(8,128)(2,1)}, u32[]{:S(2)}) copy-start(bf16[1,1792,1024]{2,1,0:T(8,128)(2,1)} %param.9) | copy-start | bytes 11010052
  74.8 1.3 copy-start.2
  76.1 1.2 copy-start.4
  77.3 43.3 %collective-permute-start.11 = (bf16[288,1024]{1,0:T(8,128)(2,1)}, bf16[288,1024]{1,0:T(8,128)(2,1)}, u32[]{:S(2)}, u32[]{:S(2)}) collective-permute-start(bf16[288,1024]{1,0:T(8,128)(2,1)} %pad_maximum_fusion.3), channel_id=1, source_target_pairs={{0,1},{1,0},{2,3},{3,2},{4,5},{5,4},{6,7},{7,6},{8,9},{9,8},{10,11... | collective-permute-start | bytes 1769480 | tf_op jit(solution)/shard_map/ppermute | solution.py:34
  82.8 16.5 %all-to-all-start.2 = ((bf16[4,72,1792]{2,1,0:T(8,128)(2,1)}), bf16[4,72,1792]{2,1,0:T(8,128)(2,1)S(1)}, u32[]{:S(2)}, u32[]{:S(2)}) async-start(bf16[4,72,1792]{2,1,0:T(8,128)(2,1)} %bitcast.9), calls=%async_computation.2 | async-start | bytes 2064384 | tf_op jit(solution)/shard_map/all_to_all | solution.py:65
  87.8 3.4 %copy-start.16 = (bf16[1,1792,1024]{2,1,0:T(8,128)(2,1)S(1)}, bf16[1,1792,1024]{2,1,0:T(8,128)(2,1)}, u32[]{:S(2)}) copy-start(bf16[1,1792,1024]{2,1,0:T(8,128)(2,1)} %param.9) | copy-start | bytes 11010052
  91.3 1.3 copy-start.6
  92.5 1.3 copy-start.8
  93.8 31.4 %collective-permute-start.7 = (bf16[288,1024]{1,0:T(8,128)(2,1)}, bf16[288,1024]{1,0:T(8,128)(2,1)}, u32[]{:S(2)}, u32[]{:S(2)}) collective-permute-start(bf16[288,1024]{1,0:T(8,128)(2,1)} %pad_maximum_fusion.2), channel_id=1, source_target_pairs={{0,1},{1,0},{2,3},{3,2},{4,5},{5,4},{6,7},{7,6},{8,9},{9,8},{10,11... | collective-permute-start | bytes 1769480 | tf_op jit(solution)/shard_map/ppermute | solution.py:34
  99.3 16.5 %all-to-all-start = ((bf16[4,72,1792]{2,1,0:T(8,128)(2,1)}), bf16[4,72,1792]{2,1,0:T(8,128)(2,1)S(1)}, u32[]{:S(2)}, u32[]{:S(2)}) async-start(bf16[4,72,1792]{2,1,0:T(8,128)(2,1)} %bitcast.1), calls=%async_computation | async-start | bytes 2064384 | tf_op jit(solution)/shard_map/all_to_all | solution.py:65
  104.3 3.4 %copy-start.17 = (bf16[1,1792,1024]{2,1,0:T(8,128)(2,1)S(1)}, bf16[1,1792,1024]{2,1,0:T(8,128)(2,1)}, u32[]{:S(2)}) copy-start(bf16[1,1792,1024]{2,1,0:T(8,128)(2,1)} %param.9) | copy-start | bytes 11010052
  109.0 1.3 copy-start.1
  110.2 24.5 %collective-permute-start.3 = (bf16[288,1024]{1,0:T(8,128)(2,1)}, bf16[288,1024]{1,0:T(8,128)(2,1)}, u32[]{:S(2)}, u32[]{:S(2)}) collective-permute-start(bf16[288,1024]{1,0:T(8,128)(2,1)} %pad_maximum_fusion.1), channel_id=1, source_target_pairs={{0,1},{1,0},{2,3},{3,2},{4,5},{5,4},{6,7},{7,6},{8,9},{9,8},{10,11... | collective-permute-start | bytes 1769480 | tf_op jit(solution)/shard_map/ppermute | solution.py:34
  115.7 3.4 %copy-start.18 = (bf16[1,1792,1024]{2,1,0:T(8,128)(2,1)S(1)}, bf16[1,1792,1024]{2,1,0:T(8,128)(2,1)}, u32[]{:S(2)}) copy-start(bf16[1,1792,1024]{2,1,0:T(8,128)(2,1)} %param.9) | copy-start | bytes 11010052
  119.2 1.4 copy-start.5
  120.5 3.2 %copy-start = (f32[288,1024]{1,0:T(8,128)}, f32[288,1024]{1,0:T(8,128)S(1)}, u32[]{:S(2)}) copy-start(f32[288,1024]{1,0:T(8,128)S(1)} %fusion.22) | copy-start | bytes 3538948
  120.5 1.7 copy-start.3
  122.2 3.0 %copy-start.9 = (f32[288,1024]{1,0:T(8,128)S(1)}, f32[288,1024]{1,0:T(8,128)}, u32[]{:S(2)}) copy-start(f32[288,1024]{1,0:T(8,128)} %copy-done.8) | copy-start | bytes 3538948
  123.7 1.5 copy-start.7
  123.7 3.8 %collective-permute-start.12 = (bf16[288,512]{1,0:T(8,128)(2,1)S(1)}, bf16[288,512]{1,0:T(8,128)(2,1)S(1)}, u32[]{:S(2)}, u32[]{:S(2)}) collective-permute-start(bf16[288,512]{1,0:T(8,128)(2,1)S(1)} %multiply_convert_fusion), channel_id=1, source_target_pairs={{0,1},{1,0},{2,3},{3,2},{4,5},{5,4},{6,7},{7,6},{8,9},{9,8},{10,11... | collective-permute-start | bytes 884744 | tf_op jit(solution)/shard_map/ppermute | solution.py:38
  124.7 28.0 %collective-permute-start = (bf16[288,1024]{1,0:T(8,128)(2,1)}, bf16[288,1024]{1,0:T(8,128)(2,1)}, u32[]{:S(2)}, u32[]{:S(2)}) collective-permute-start(bf16[288,1024]{1,0:T(8,128)(2,1)} %pad_maximum_fusion), channel_id=1, source_target_pairs={{0,1},{1,0},{2,3},{3,2},{4,5},{5,4},{6,7},{7,6},{8,9},{9,8},{10,11... | collective-permute-start | bytes 1769480 | tf_op jit(solution)/shard_map/ppermute | solution.py:34
  125.2 2.4 %copy-start.19 = (bf16[1,1024,1792]{2,1,0:T(8,128)(2,1)S(1)}, bf16[1,1024,1792]{2,1,0:T(8,128)(2,1)}, u32[]{:S(2)}) copy-start(bf16[1,1024,1792]{2,1,0:T(8,128)(2,1)} %param.11) | copy-start | bytes 11010052
  127.5 10.1 %collective-permute-start.8 = (bf16[288,512]{1,0:T(8,128)(2,1)}, bf16[288,512]{1,0:T(8,128)(2,1)}, u32[]{:S(2)}, u32[]{:S(2)}) collective-permute-start(bf16[288,512]{1,0:T(8,128)(2,1)} %multiply_convert_fusion.1), channel_id=1, source_target_pairs={{0,1},{1,0},{2,3},{3,2},{4,5},{5,4},{6,7},{7,6},{8,9},{9,8},{10,11... | collective-permute-start | bytes 884744 | tf_op jit(solution)/shard_map/ppermute | solution.py:38
  129.8 17.9 %all-to-all-start.7 = ((bf16[4,72,1792]{2,1,0:T(8,128)(2,1)}), bf16[4,72,1792]{2,1,0:T(8,128)(2,1)S(1)}, u32[]{:S(2)}, u32[]{:S(2)}) async-start(bf16[4,72,1792]{2,1,0:T(8,128)(2,1)} %bitcast.97), calls=%async_computation.7 | async-start | bytes 2064384 | tf_op jit(solution)/shard_map/all_to_all | solution.py:65
  134.8 3.9 %copy-start.20 = (bf16[1,1024,1792]{2,1,0:T(8,128)(2,1)S(1)}, bf16[1,1024,1792]{2,1,0:T(8,128)(2,1)}, u32[]{:S(2)}) copy-start(bf16[1,1024,1792]{2,1,0:T(8,128)(2,1)} %param.11) | copy-start | bytes 11010052
  137.4 17.2 %collective-permute-start.4 = (bf16[288,512]{1,0:T(8,128)(2,1)}, bf16[288,512]{1,0:T(8,128)(2,1)}, u32[]{:S(2)}, u32[]{:S(2)}) collective-permute-start(bf16[288,512]{1,0:T(8,128)(2,1)} %multiply_convert_fusion.2), channel_id=1, source_target_pairs={{0,1},{1,0},{2,3},{3,2},{4,5},{5,4},{6,7},{7,6},{8,9},{9,8},{10,11... | collective-permute-start | bytes 884744 | tf_op jit(solution)/shard_map/ppermute | solution.py:38
  147.7 17.0 %all-to-all-start.5 = ((bf16[4,72,1792]{2,1,0:T(8,128)(2,1)}), bf16[4,72,1792]{2,1,0:T(8,128)(2,1)S(1)}, u32[]{:S(2)}, u32[]{:S(2)}) async-start(bf16[4,72,1792]{2,1,0:T(8,128)(2,1)} %bitcast.94), calls=%async_computation.5 | async-start | bytes 2064384 | tf_op jit(solution)/shard_map/all_to_all | solution.py:65
  152.7 3.1 %copy-start.21 = (bf16[1,1024,1792]{2,1,0:T(8,128)(2,1)S(1)}, bf16[1,1024,1792]{2,1,0:T(8,128)(2,1)}, u32[]{:S(2)}) copy-start(bf16[1,1024,1792]{2,1,0:T(8,128)(2,1)} %param.11) | copy-start | bytes 11010052
  154.6 15.1 %collective-permute-start.1 = (bf16[288,512]{1,0:T(8,128)(2,1)S(1)}, bf16[288,512]{1,0:T(8,128)(2,1)}, u32[]{:S(2)}, u32[]{:S(2)}) collective-permute-start(bf16[288,512]{1,0:T(8,128)(2,1)S(1)} %multiply_convert_fusion.3), channel_id=1, source_target_pairs={{0,1},{1,0},{2,3},{3,2},{4,5},{5,4},{6,7},{7,6},{8,9},{9,8},{10,11... | collective-permute-start | bytes 884744 | tf_op jit(solution)/shard_map/ppermute | solution.py:38
  164.7 16.5 %all-to-all-start.3 = ((bf16[4,72,1792]{2,1,0:T(8,128)(2,1)}), bf16[4,72,1792]{2,1,0:T(8,128)(2,1)S(1)}, u32[]{:S(2)}, u32[]{:S(2)}) async-start(bf16[4,72,1792]{2,1,0:T(8,128)(2,1)} %bitcast.96), calls=%async_computation.3 | async-start | bytes 2064384 | tf_op jit(solution)/shard_map/all_to_all | solution.py:65
  170.7 4.3 %copy-start.14 = (bf16[128,4]{0,1:T(4,128)(2,1)S(1)}, bf16[128,4]{0,1:T(4,128)(2,1)}, u32[]{:S(2)}) copy-start(bf16[128,4]{0,1:T(4,128)(2,1)} %get-tuple-element.6) | copy-start | bytes 3076
  176.2 10.0 %copy-start.13 = (bf16[128,4]{0,1:T(4,128)(2,1)S(1)}, bf16[128,4]{0,1:T(4,128)(2,1)}, u32[]{:S(2)}) copy-start(bf16[128,4]{0,1:T(4,128)(2,1)} %get-tuple-element.7) | copy-start | bytes 3076
  176.2 21.5 %collective-permute-start.13 = (bf16[128,1792]{1,0:T(8,128)(2,1)}, bf16[128,1792]{1,0:T(8,128)(2,1)}, u32[]{:S(2)}, u32[]{:S(2)}) collective-permute-start(bf16[128,1792]{1,0:T(8,128)(2,1)} %fusion.38), channel_id=1, source_target_pairs={{0,24},{2,26},{4,28},{6,30},{8,16},{10,18},{12,20},{14,22},{16,8},... | collective-permute-start | bytes 1376264 | tf_op jit(solution)/shard_map/ppermute | solution.py:112
  181.2 16.6 %all-to-all-start.1 = ((bf16[4,72,1792]{2,1,0:T(8,128)(2,1)}), bf16[4,72,1792]{2,1,0:T(8,128)(2,1)S(1)}, u32[]{:S(2)}, u32[]{:S(2)}) async-start(bf16[4,72,1792]{2,1,0:T(8,128)(2,1)} %bitcast.95), calls=%async_computation.1 | async-start | bytes 2064384 | tf_op jit(solution)/shard_map/all_to_all | solution.py:65
  186.2 1.3 copy-start.12
  186.2 23.7 %copy-start.11 = (bf16[128,4]{0,1:T(4,128)(2,1)S(1)}, bf16[128,4]{0,1:T(4,128)(2,1)}, u32[]{:S(2)}) copy-start(bf16[128,4]{0,1:T(4,128)(2,1)} %get-tuple-element.5) | copy-start | bytes 3076
  187.4 19.3 %collective-permute-start.9 = (bf16[128,1792]{1,0:T(8,128)(2,1)}, bf16[128,1792]{1,0:T(8,128)(2,1)S(1)}, u32[]{:S(2)}, u32[]{:S(2)}) collective-permute-start(bf16[128,1792]{1,0:T(8,128)(2,1)} %fusion.37), channel_id=1, source_target_pairs={{0,16},{2,18},{4,20},{6,22},{8,24},{10,26},{12,28},{14,30},{16,0},... | collective-permute-start | bytes 1376264 | tf_op jit(solution)/shard_map/ppermute | solution.py:112
  187.9 22.0 %collective-permute-start.5 = (bf16[128,1792]{1,0:T(8,128)(2,1)S(1)}, bf16[128,1792]{1,0:T(8,128)(2,1)S(1)}, u32[]{:S(2)}, u32[]{:S(2)}) collective-permute-start(bf16[128,1792]{1,0:T(8,128)(2,1)S(1)} %fusion.36), channel_id=1, source_target_pairs={{0,8},{2,10},{4,12},{6,14},{8,0},{10,2},{12,4},{14,6},{16,24},{18,... | collective-permute-start | bytes 1376264 | tf_op jit(solution)/shard_map/ppermute | solution.py:112
